TPU v7x, 32 devices: a whole 2x2x4 slice. The times are simulated.
32 devices in a mesh: rows: 8 (over y, x, core), feat: 4 (over z).
Axes of the slice: x: 2, y: 2, z: 4, core: 2. Of those that a mesh axis runs over, the one named last changes fastest.
Arguments:
- bins: int32 [8192, 512], P('rows', 'feat'), may hold values from -2147483648 to 2147483647, as said below
- hessian: float32 [32768], P('rows'), may hold values from 0.05 to 1
- thresholds: float32 [128], replicated, may hold values from 0.02 to 0.98
Outputs:
- cuts: float32 [512, 128], P('feat')
Inputs may be any that keep to these rules, and one draw needn't show every extreme that they name: `bins`: each word holds the bin ids, 0 to 255, of rows 4i to 4i + 3 of one feature, row 4i + k in bits 8k to 8k + 7 of the two's complement word.
All inputs are finite; a program needn't handle non-finite values.
Results may differ from a plain program's by a relative error of at most 0.000065.
Values sent between devices are 32-bit elements; how exact they have to be, the bound alone decides.
A program may use at most 192 MiB of HBM per device.

v0:
```python
import math

import jax
import jax.numpy as jnp
from jax import lax
from jax.sharding import PartitionSpec as P

BINS = 256


def unpack(words):
    parts = [jnp.bitwise_and(jnp.right_shift(words, 8 * k), 255) for k in range(4)]
    stacked = jnp.stack(parts, axis=1)
    return stacked.reshape(words.shape[0] * 4, words.shape[1])


def histogram(columns, weights):
    count, width = columns.shape
    limit = max(8, 1048576 // (width * 16))
    block = math.gcd(count, limit)
    col_blocks = columns.reshape(count // block, block, width)
    wt_blocks = weights.reshape(count // block, block)
    levels = jnp.arange(16, dtype=jnp.int32)

    def add_block(total, item):
        col_part, wt_part = item
        high = jnp.right_shift(col_part, 4)
        low = jnp.bitwise_and(col_part, 15)
        high_hot = jnp.where(high[:, :, None] == levels, wt_part[:, None, None], 0.0)
        low_hot = (low[:, :, None] == levels).astype(jnp.float32)
        joint = jnp.einsum("rkh,rkl->khl", high_hot, low_hot, precision=lax.Precision.HIGHEST)
        return (total + joint, None)

    start = jnp.zeros((width, 16, 16), jnp.float32)
    total, unused = lax.scan(add_block, start, (col_blocks, wt_blocks))
    return total.reshape(width, BINS)


def cut_positions(hist, thresholds):
    cum = jnp.cumsum(hist, axis=1)
    before = cum - hist
    total = cum[:, -1]
    target = thresholds[None, :, None] * total[:, None, None]
    ratio = (target - before[:, None, :]) / (hist[:, None, :] + 1.0)
    return jnp.sum(jnp.clip(ratio, 0.0, 1.0), axis=2)


def local(bins, hessian, thresholds):
    regrouped = lax.all_to_all(bins, "rows", split_axis=1, concat_axis=0, tiled=True)
    weights = lax.all_gather(hessian, "rows", axis=0, tiled=True)
    hist = histogram(unpack(regrouped), weights)
    cuts = cut_positions(hist, thresholds)
    return lax.all_gather(cuts, "rows", axis=0, tiled=True)


def solution(mesh):
    in_specs = (P("rows", "feat"), P("rows"), P())
    out_specs = P("feat", None)
    return jax.shard_map(local, mesh=mesh, in_specs=in_specs, out_specs=out_specs, check_vma=False)
```

profile of v0, /device:TPU:0, one launch (start us, length us, event | category | flops | bytes accessed | tf_op | source)
XLA Modules:
  0.0 84.6 jit_solution(17974510913110473244)
XLA Ops:
  0.0 2.0 %copy.34 = s32[1024,128]{0,1:T(8,128)} copy(s32[1024,128]{1,0:T(8,128)} %param.5) | data formatting | bytes 1048576 | tf_op args[0]
  2.0 5.2 %all-to-all-start = ((s32[1024,8,16]{0,2,1:T(8,128)}), s32[1024,8,16]{0,2,1:T(8,128)S(1)}, u32[]{:S(2)}, u32[]{:S(2)}) async-start(s32[1024,8,16]{0,2,1:T(8,128)} %bitcast), calls=%async_computation | async-start | bytes 1048576 | tf_op jit(solution)/shard_map/all_to_all | solution.py:49
  7.3 13.2 %all_gather.6 = f32[32768]{0:T(1024)S(1)} all-gather(f32[4096]{0:T(1024)S(1)} %copy-done), channel_id=1, replica_groups=mesh['rows'=8,'feat'=4] {'rows'}, dimensions={0}, use_global_device_ids=true | all-gather | bytes 147456 | tf_op jit(solution)/shard_map/all_gather | solution.py:50
  20.5 0.3 and_bitcast_fusion.4
  20.7 0.3 copy.35
  21.1 0.1 and.76
  21.2 0.3 copy.36
  21.5 0.1 and.79
  21.6 0.3 copy.37
  21.9 0.9 %and.82 = s32[8192,1,16]{0,2,1:T(8,128)} reshape(s32[8,1024,16]{1,0,2:T(8,128)S(1)} %copy.37) | data formatting | bytes 1048576 | tf_op jit(solution)/shard_map/and | solution.py:12
  22.8 0.3 copy.38
  23.1 0.9 %and.85 = s32[8192,1,16]{0,2,1:T(8,128)} reshape(s32[8,1024,16]{1,0,2:T(8,128)S(1)} %copy.38) | data formatting | bytes 1048576 | tf_op jit(solution)/shard_map/and | solution.py:12
  24.0 1.3 %pad_add_fusion = s32[8192,4,16]{0,2,1:T(8,128)S(1)} fusion(s32[8192,1,16]{0,2,1:T(8,128)} %and.85, s32[8192,1,16]{0,2,1:T(8,128)} %and.82, s32[8192,1,16]{0,2,1:T(8,128)S(1)} %and.79, s32[8192,1,16]{0,2,1:T(8,128)S(1)} %and.76), kind=kLoop, calls=%fused_computation.14 | loop fusion | flops 1572864 | bytes 4194304 | tf_op jit(solution)/shard_map/stack | solution.py:13
  25.4 10.7 %copy.39 = s32[8192,4,16]{2,1,0:T(4,128)} copy(s32[8192,4,16]{0,2,1:T(8,128)S(1)} %pad_add_fusion) | data formatting | bytes 4194304 | tf_op jit(solution)/shard_map/stack | solution.py:13
  36.1 9.6 %copy.40 = s32[8,4096,16]{1,2,0:T(8,128)S(1)} copy(s32[8,4096,16]{2,1,0:T(8,128)} %bitcast.35) | data formatting | bytes 4194304
  45.7 27.9 %while.12 = (s32[]{:T(128)}, f32[16,16,16]{2,1,0:T(8,128)S(1)}, s32[8,4096,16]{1,2,0:T(8,128)S(1)}, f32[8,4096]{1,0:T(8,128)S(1)}, s32[]{:T(128)}, /*index=5*/s32[]{:T(128)}) while((s32[]{:T(128)}, f32[16,16,16]{2,1,0:T(8,128)S(1)}, s32[8,4096,16]{1,2,0:T(8,128)S(1)}, f32[8,4096]{1,0:T(8,128)S(1)}, s32[]{:T(128)}, ...), condition=%wide.region_1.2_spmd.clone.clone, body=%wide.region_0.1_spmd.clone.clone.sunk | while | flops 204611584 | bytes 1392727 | solution.py:35
  45.8 3.4 %fusion.16 = f32[16,16,16]{2,1,0:T(8,128)S(1)} fusion(s32[4096,16]{0,1:T(8,128)S(1)} %get-tuple-element.126, f32[4096]{0:T(1024)S(1)} %bitcast.36, s32[4096,16]{0,1:T(8,128)S(1)} %get-tuple-element.127, f32[16,16,16]{2,1,0:T(8,128)S(1)} %get-tuple-element.135, pred[]{:T(512)S(6)} %compare.3), kind=kOutput, calls=%fused_computation.9.clone.1 | convolution fusion | flops 204480512 | bytes 573441 | tf_op jit(solution)/shard_map/while/body/eval_jaxpr/rkh,rkl->khl/dot_general | solution.py:31
  49.3 3.4 %fusion.16 = f32[16,16,16]{2,1,0:T(8,128)S(1)} fusion(s32[4096,16]{0,1:T(8,128)S(1)} %get-tuple-element.126, f32[4096]{0:T(1024)S(1)} %bitcast.36, s32[4096,16]{0,1:T(8,128)S(1)} %get-tuple-element.127, f32[16,16,16]{2,1,0:T(8,128)S(1)} %get-tuple-element.135, pred[]{:T(512)S(6)} %compare.3), kind=kOutput, calls=%fused_computation.9.clone.1 | convolution fusion | flops 204480512 | bytes 573441 | tf_op jit(solution)/shard_map/while/body/eval_jaxpr/rkh,rkl->khl/dot_general | solution.py:31
  52.8 3.4 %fusion.16 = f32[16,16,16]{2,1,0:T(8,128)S(1)} fusion(s32[4096,16]{0,1:T(8,128)S(1)} %get-tuple-element.126, f32[4096]{0:T(1024)S(1)} %bitcast.36, s32[4096,16]{0,1:T(8,128)S(1)} %get-tuple-element.127, f32[16,16,16]{2,1,0:T(8,128)S(1)} %get-tuple-element.135, pred[]{:T(512)S(6)} %compare.3), kind=kOutput, calls=%fused_computation.9.clone.1 | convolution fusion | flops 204480512 | bytes 573441 | tf_op jit(solution)/shard_map/while/body/eval_jaxpr/rkh,rkl->khl/dot_general | solution.py:31
  56.2 3.4 %fusion.16 = f32[16,16,16]{2,1,0:T(8,128)S(1)} fusion(s32[4096,16]{0,1:T(8,128)S(1)} %get-tuple-element.126, f32[4096]{0:T(1024)S(1)} %bitcast.36, s32[4096,16]{0,1:T(8,128)S(1)} %get-tuple-element.127, f32[16,16,16]{2,1,0:T(8,128)S(1)} %get-tuple-element.135, pred[]{:T(512)S(6)} %compare.3), kind=kOutput, calls=%fused_computation.9.clone.1 | convolution fusion | flops 204480512 | bytes 573441 | tf_op jit(solution)/shard_map/while/body/eval_jaxpr/rkh,rkl->khl/dot_general | solution.py:31
  59.7 3.4 %fusion.16 = f32[16,16,16]{2,1,0:T(8,128)S(1)} fusion(s32[4096,16]{0,1:T(8,128)S(1)} %get-tuple-element.126, f32[4096]{0:T(1024)S(1)} %bitcast.36, s32[4096,16]{0,1:T(8,128)S(1)} %get-tuple-element.127, f32[16,16,16]{2,1,0:T(8,128)S(1)} %get-tuple-element.135, pred[]{:T(512)S(6)} %compare.3), kind=kOutput, calls=%fused_computation.9.clone.1 | convolution fusion | flops 204480512 | bytes 573441 | tf_op jit(solution)/shard_map/while/body/eval_jaxpr/rkh,rkl->khl/dot_general | solution.py:31
  63.2 3.4 %fusion.16 = f32[16,16,16]{2,1,0:T(8,128)S(1)} fusion(s32[4096,16]{0,1:T(8,128)S(1)} %get-tuple-element.126, f32[4096]{0:T(1024)S(1)} %bitcast.36, s32[4096,16]{0,1:T(8,128)S(1)} %get-tuple-element.127, f32[16,16,16]{2,1,0:T(8,128)S(1)} %get-tuple-element.135, pred[]{:T(512)S(6)} %compare.3), kind=kOutput, calls=%fused_computation.9.clone.1 | convolution fusion | flops 204480512 | bytes 573441 | tf_op jit(solution)/shard_map/while/body/eval_jaxpr/rkh,rkl->khl/dot_general | solution.py:31
  66.7 3.4 %fusion.16 = f32[16,16,16]{2,1,0:T(8,128)S(1)} fusion(s32[4096,16]{0,1:T(8,128)S(1)} %get-tuple-element.126, f32[4096]{0:T(1024)S(1)} %bitcast.36, s32[4096,16]{0,1:T(8,128)S(1)} %get-tuple-element.127, f32[16,16,16]{2,1,0:T(8,128)S(1)} %get-tuple-element.135, pred[]{:T(512)S(6)} %compare.3), kind=kOutput, calls=%fused_computation.9.clone.1 | convolution fusion | flops 204480512 | bytes 573441 | tf_op jit(solution)/shard_map/while/body/eval_jaxpr/rkh,rkl->khl/dot_general | solution.py:31
  70.2 3.4 %fusion.16 = f32[16,16,16]{2,1,0:T(8,128)S(1)} fusion(s32[4096,16]{0,1:T(8,128)S(1)} %get-tuple-element.126, f32[4096]{0:T(1024)S(1)} %bitcast.36, s32[4096,16]{0,1:T(8,128)S(1)} %get-tuple-element.127, f32[16,16,16]{2,1,0:T(8,128)S(1)} %get-tuple-element.135, pred[]{:T(512)S(6)} %compare.3), kind=kOutput, calls=%fused_computation.9.clone.1 | convolution fusion | flops 204480512 | bytes 573441 | tf_op jit(solution)/shard_map/while/body/eval_jaxpr/rkh,rkl->khl/dot_general | solution.py:31
  73.6 0.1 reshape.161
  73.7 0.1 reshape.163
  73.8 0.6 reduce-window.6
  74.4 0.2 slice_reduce_fusion
  74.8 0.2 slice_reduce_fusion.1
  75.0 0.7 clamp_reduce_fusion
  75.7 8.3 %all_gather.7 = f32[128,128]{1,0:T(8,128)S(1)} all-gather(f32[16,128]{1,0:T(8,128)S(1)} %clamp_reduce_fusion), channel_id=1, replica_groups=mesh['rows'=8,'feat'=4] {'rows'}, dimensions={0}, use_global_device_ids=true | all-gather | bytes 73728 | tf_op jit(solution)/shard_map/all_gather | solution.py:53
  84.0 0.6 copy.54
  (29 shorter events, 0.8 us)
Async XLA Ops:
  0.0 7.2 %copy-start = (f32[4096]{0:T(1024)S(1)}, f32[4096]{0:T(1024)}, u32[]{:S(2)}) copy-start(f32[4096]{0:T(1024)} %param.6) | copy-start | bytes 49156
  2.0 18.4 %all-to-all-start = ((s32[1024,8,16]{0,2,1:T(8,128)}), s32[1024,8,16]{0,2,1:T(8,128)S(1)}, u32[]{:S(2)}, u32[]{:S(2)}) async-start(s32[1024,8,16]{0,2,1:T(8,128)} %bitcast), calls=%async_computation | async-start | bytes 1048576 | tf_op jit(solution)/shard_map/all_to_all | solution.py:49
  45.7 29.3 %copy-start.1 = (f32[128]{0:T(128)S(1)}, f32[128]{0:T(128)}, u32[]{:S(2)}) copy-start(f32[128]{0:T(128)} %param.7) | copy-start | bytes 1540
where the time goes:
time: 85 us; the launch traced here: 84.6 us
  matrix products  27.1 us (32%)
  local copies, waits for them, and re-layouts  27 us (32%)
  blocking collectives  21.5 us (25%)
  starting transfers between devices  5.2 us (6%)
  other arithmetic  3.46 us (4%)
    dot_general x8, matrix products, add_block(): jnp.einsum('rkh,rkl->khl', high_hot, low_hot, precision=lax.Precision.HIG...  27.1 us
    all_gather x1, blocking collectives, local(): weights = lax.all_gather(hessian, 'rows', axis=0, tiled=True)  13.2 us
    unnamed x7, local copies, waits for them, and re-layouts  12.3 us
    another operation x1, local copies, waits for them, and re-layouts, unpack(): stacked = jnp.stack(parts, axis=1)  10.7 us
    all_gather x1, blocking collectives, local(): return lax.all_gather(cuts, 'rows', axis=0, tiled=True)  8.29 us
    all_to_all x1, starting transfers between devices, local(): lax.all_to_all(bins, 'rows', split_axis=1, concat_axis=0, tiled=True)  5.2 us
    and x8, local copies, waits for them, and re-layouts, unpack(): jnp.bitwise_and(jnp.right_shift(words, 8 * k), 255)  3.23 us
  transfers between devices with their start and end apart: 1, of which 0 were waited for; matrix products, arithmetic and copies ran while one was open for 0% of the time, Pallas kernels for 0%

commit v1 on v0

v1 whole, which is shorter than its diff:
```python
import functools

import jax
import jax.numpy as jnp
from jax import lax
from jax.experimental import pallas as pl
from jax.experimental.pallas import tpu as pltpu
from jax.sharding import PartitionSpec as P

BINS = 256
LEVELS = 16
GROUP = 16
LANES = 128
CHUNK = 256
MESH = pl.DeviceIdType.MESH


def kernel(ranks, bins_ref, hess_ref, thr_ref, out_ref, cols, wts, stage, inbox, mine, send_sem, recv_sem, gather_send, gather_recv):
    words, width = bins_ref.shape
    groups = width // GROUP
    replicas = ranks // groups
    lanes = LEVELS * GROUP
    me = lax.axis_index("rows")
    team, seat = me // groups, me % groups

    barrier = pltpu.get_barrier_semaphore()
    for step in range(1, ranks):
        pl.semaphore_signal(barrier, inc=1, device_id={"rows": (me + step) % ranks}, device_id_type=MESH)

    span = 4 * LANES
    tiles = words // LANES
    flat = jnp.concatenate([hess_ref[pl.ds(j, tiles, stride=4), :] for j in range(4)], axis=1)
    top = flat.astype(jnp.bfloat16).astype(jnp.float32)
    rest = flat - top
    row = lax.broadcasted_iota(jnp.int32, (span, span), 0)
    col = lax.broadcasted_iota(jnp.int32, (span, span), 1)
    order = jnp.where(row == 4 * (col % LANES) + col // LANES, 1.0, 0.0).astype(jnp.bfloat16)
    pieces = jnp.concatenate([top, rest], axis=0).astype(jnp.bfloat16)
    moved = jnp.dot(pieces, order, preferred_element_type=jnp.float32)
    for piece in range(2):
        for k in range(4):
            for t in range(tiles):
                line = moved[piece * tiles + t : piece * tiles + t + 1, k * LANES : (k + 1) * LANES]
                wts[piece, k, :, t * LANES : (t + 1) * LANES] = jnp.broadcast_to(line, (GROUP, LANES)).astype(jnp.bfloat16)

    for t in range(tiles):
        cols[:, t * LANES : (t + 1) * LANES] = bins_ref[t * LANES : (t + 1) * LANES, :].T

    def group_hist(group):
        base = pl.multiple_of(group * GROUP, GROUP)
        zero = jnp.zeros((GROUP, CHUNK), jnp.bfloat16)
        one = jnp.ones((GROUP, CHUNK), jnp.bfloat16)
        sums = [None, None]
        index = 0
        for c in range(words // CHUNK):
            part = cols[pl.ds(base, GROUP), c * CHUNK : (c + 1) * CHUNK]
            for k in range(4):
                high = jnp.bitwise_and(jnp.right_shift(part, 8 * k + 4), 15).astype(jnp.float32).astype(jnp.bfloat16)
                low = jnp.bitwise_and(jnp.right_shift(part, 8 * k), 15).astype(jnp.float32).astype(jnp.bfloat16)
                w0 = wts[0, k, :, c * CHUNK : (c + 1) * CHUNK]
                w1 = wts[1, k, :, c * CHUNK : (c + 1) * CHUNK]
                hot = [high == jnp.bfloat16(h) for h in range(LEVELS)]
                left = jnp.concatenate([jnp.where(m, w0, zero) for m in hot] + [jnp.where(m, w1, zero) for m in hot], axis=0)
                right = jnp.concatenate([jnp.where(low == jnp.bfloat16(l), one, zero) for l in range(LEVELS)], axis=0)
                part_sum = lax.dot_general(left, right, (((1,), (1,)), ((), ())), preferred_element_type=jnp.float32)
                side = index % 2
                sums[side] = part_sum if sums[side] is None else sums[side] + part_sum
                index += 1
        both = sums[0] + sums[1]
        joint = both[:lanes] + both[lanes:]
        own_row = lax.broadcasted_iota(jnp.int32, (GROUP, lanes), 0)
        own_col = lax.broadcasted_iota(jnp.int32, (GROUP, lanes), 1)
        keep = own_row == own_col % GROUP
        lines = []
        for h in range(LEVELS):
            lines.append(jnp.sum(jnp.where(keep, joint[h * GROUP : (h + 1) * GROUP], 0.0), axis=0, keepdims=True))
        return jnp.concatenate(lines, axis=0)

    def outgoing(step, e):
        target = ((team + e) % replicas) * groups + (seat + step) % groups
        slot = step * replicas + e
        return pltpu.make_async_remote_copy(
            src_ref=stage.at[step],
            dst_ref=inbox.at[slot],
            send_sem=send_sem.at[slot],
            recv_sem=recv_sem.at[slot],
            device_id={"rows": target},
            device_id_type=MESH,
        )

    def do_group(turn, carry):
        step = (turn + 1) % groups
        stage[step] = group_hist((seat + step) % groups)

        @pl.when(turn == 0)
        def _():
            pl.semaphore_wait(barrier, ranks - 1)

        @pl.when(turn < groups - 1)
        def _():
            for e in range(replicas):
                outgoing(step, e).start()

        return carry

    lax.fori_loop(0, groups, do_group, 0)
    for e in range(1, replicas):
        outgoing(0, e).start()

    total = stage[0]
    for step in range(groups):
        for e in range(replicas):
            if step + e > 0:
                outgoing(step, e).wait()
                total = total + inbox[step * replicas + e]

    src = lax.broadcasted_iota(jnp.int32, (lanes, lanes), 0)
    dst = lax.broadcasted_iota(jnp.int32, (lanes, lanes), 1)
    same = src % GROUP == dst % GROUP
    earlier = jnp.where(jnp.logical_and(same, src < dst), 1.0, 0.0).astype(jnp.bfloat16)
    every = jnp.where(same, 1.0, 0.0).astype(jnp.bfloat16)
    p0 = total.astype(jnp.bfloat16).astype(jnp.float32)
    p1 = (total - p0).astype(jnp.bfloat16).astype(jnp.float32)
    p2 = total - p0 - p1
    split = jnp.concatenate([p0, p1, p2], axis=0).astype(jnp.bfloat16)
    inner3 = jnp.dot(split, earlier, preferred_element_type=jnp.float32)
    level3 = jnp.dot(split, every, preferred_element_type=jnp.float32)
    inner = inner3[:LEVELS] + inner3[LEVELS : 2 * LEVELS] + inner3[2 * LEVELS :]
    level = level3[:LEVELS] + level3[LEVELS : 2 * LEVELS] + level3[2 * LEVELS :]
    inv = 1.0 / (total + 1.0)
    column = jnp.broadcast_to(thr_ref[...], (LANES, thr_ref.shape[1])).T
    whole = jnp.sum(level, axis=0, keepdims=True)
    target = column * whole[:, :LANES]
    run = jnp.zeros((1, lanes), jnp.float32)
    acc = jnp.zeros((thr_ref.shape[1], LANES), jnp.float32)
    for h in range(LEVELS):
        before = inner[h : h + 1] + run
        run = run + level[h : h + 1]
        for t in range(lanes // LANES):
            cut = slice(t * LANES, (t + 1) * LANES)
            ratio = (target - before[:, cut]) * inv[h : h + 1, cut]
            acc = acc + jnp.clip(ratio, 0.0, 1.0)
    turned = acc.T
    cuts = turned[:GROUP]
    for j in range(1, LANES // GROUP):
        cuts = cuts + turned[j * GROUP : (j + 1) * GROUP]
    mine[...] = cuts
    here = pl.multiple_of(seat * GROUP, GROUP)

    def spread(step):
        return pltpu.make_async_remote_copy(
            src_ref=mine,
            dst_ref=out_ref.at[pl.ds(here, GROUP), :],
            send_sem=gather_send.at[step],
            recv_sem=gather_recv.at[step],
            device_id={"rows": team * groups + (seat + step) % groups},
            device_id_type=MESH,
        )

    for step in range(1, groups):
        spread(step).start()
    out_ref[pl.ds(here, GROUP), :] = cuts
    for step in range(1, groups):
        spread(step).wait()


def solution(mesh):
    ranks = mesh.shape["rows"]

    def local(bins, hessian, thresholds):
        words, width = bins.shape
        groups = width // GROUP
        quantiles = thresholds.shape[0]
        lanes = LEVELS * GROUP
        return pl.pallas_call(
            functools.partial(kernel, ranks),
            out_shape=jax.ShapeDtypeStruct((width, quantiles), jnp.float32),
            in_specs=[pl.BlockSpec(memory_space=pltpu.VMEM)] * 3,
            out_specs=pl.BlockSpec(memory_space=pltpu.VMEM),
            scratch_shapes=[
                pltpu.VMEM((width, words), jnp.int32),
                pltpu.VMEM((2, 4, GROUP, words), jnp.bfloat16),
                pltpu.VMEM((groups, LEVELS, lanes), jnp.float32),
                pltpu.VMEM((ranks, LEVELS, lanes), jnp.float32),
                pltpu.VMEM((GROUP, quantiles), jnp.float32),
                pltpu.SemaphoreType.DMA((ranks,)),
                pltpu.SemaphoreType.DMA((ranks,)),
                pltpu.SemaphoreType.DMA((groups,)),
                pltpu.SemaphoreType.DMA((groups,)),
            ],
            compiler_params=pltpu.CompilerParams(collective_id=0, has_side_effects=True),
        )(bins, hessian.reshape(-1, LANES), thresholds.reshape(1, -1))

    in_specs = (P("rows", "feat"), P("rows"), P())
    return jax.shard_map(local, mesh=mesh, in_specs=in_specs, out_specs=P("feat", None), check_vma=False)
```

time: 85 us -> 21.4 us (0.25)
  matrix products: 27.1 us -> 0 us
  local copies, waits for them, and re-layouts: 27 us -> 1.47 us
  blocking collectives: 21.5 us -> 0 us
  Pallas kernels: 0 us -> 19.7 us
  starting transfers between devices: 5.2 us -> 0 us
  other arithmetic: 3.46 us -> 0 us
    dot_general x8 -> x0, matrix products: 27.1 us -> none  [add_block(): jnp.einsum('rkh,rkl->khl', high_hot, low_hot, precision=lax.Precision.HIG...]
    all_gather x2 -> x0, blocking collectives: 21.5 us -> none  [the longest x1 13.2 us: local(): weights = lax.all_gather(hessian, 'rows', axis=0, tiled=True)]
    pallas_call x0 -> x1, Pallas kernels: none -> 19.7 us  [local(): pl.pallas_call(functools.partial(kernel, ranks), out_shape=jax.ShapeDtype...]
    unnamed x7 -> x1, local copies, waits for them, and re-layouts: 12.3 us -> 1.47 us
    another operation x2 -> x0, local copies, waits for them, and re-layouts: 10.7 us -> none  [the longest x1 10.7 us: unpack(): stacked = jnp.stack(parts, axis=1)]
    all_to_all x1 -> x0, starting transfers between devices: 5.2 us -> none  [local(): lax.all_to_all(bins, 'rows', split_axis=1, concat_axis=0, tiled=True)]
    and x8 -> x0, local copies, waits for them, and re-layouts: 3.23 us -> none  [unpack(): jnp.bitwise_and(jnp.right_shift(words, 8 * k), 255)]
    another operation x4 -> x0, other arithmetic: 2.05 us -> none  [the longest x1 1.35 us: unpack(): stacked = jnp.stack(parts, axis=1)]
  transfers between devices with their start and end apart: 1 -> 0, of which waited for: 0 -> 0; matrix products, arithmetic and copies ran while one was open for 0% -> 0% of each run, Pallas kernels for 0% -> 0%
where the time goes in v1:
time: 21.4 us; the launch traced here: 21.2 us
  Pallas kernels  19.7 us (92%)
  local copies, waits for them, and re-layouts  1.47 us (7%)
    pallas_call x1, Pallas kernels, local(): pl.pallas_call(functools.partial(kernel, ranks), out_shape=jax.ShapeDtype...  19.7 us
    unnamed x1, local copies, waits for them, and re-layouts  1.47 us

profile of v1, /device:TPU:0, one launch (start us, length us, event | category | flops | bytes accessed | tf_op | source)
XLA Modules:
  0.0 21.2 jit_solution(7140573643309446936)
XLA Ops:
  0.0 19.7 %shard_map.37 = f32[128,128]{1,0:T(8,128)} custom-call(s32[1024,128]{1,0:T(8,128)} %bins_ref.1, f32[32,128]{1,0:T(8,128)} %bitcast.2, f32[1,128]{1,0:T(1,128)} %bitcast.3), custom_call_target="tpu_custom_call" | custom-call | tf_op jit(solution)/shard_map/pallas_call | solution.py:175
  19.7 1.5 %copy.5 = f32[128,128]{1,0:T(8,128)} copy(f32[128,128]{1,0:T(8,128)} %shard_map.37) | data formatting | bytes 131072

commit v2 on v1

--- a/solution.py
+++ b/solution.py
@@ -15,8 +15,18 @@
 MESH = pl.DeviceIdType.MESH
 
 
-def kernel(ranks, bins_ref, hess_ref, thr_ref, out_ref, cols, wts, stage, inbox, mine, send_sem, recv_sem, gather_send, gather_recv):
+def kernel(ranks, bins_hbm, hess_hbm, thr_hbm, out_ref, bins_ref, hess_ref, thr_ref, cols, wts, stage, inbox, mine, load_sem, send_sem, recv_sem, gather_send, gather_recv):
     words, width = bins_ref.shape
+    tiles = words // LANES
+    hess_load = pltpu.make_async_copy(hess_hbm, hess_ref, load_sem.at[tiles])
+    hess_load.start()
+    bins_loads = []
+    for t in range(tiles):
+        part = pl.ds(t * LANES, LANES)
+        bins_loads.append(pltpu.make_async_copy(bins_hbm.at[part, :], bins_ref.at[part, :], load_sem.at[t]))
+        bins_loads[t].start()
+    thr_load = pltpu.make_async_copy(thr_hbm, thr_ref, load_sem.at[tiles + 1])
+    thr_load.start()
     groups = width // GROUP
     replicas = ranks // groups
     lanes = LEVELS * GROUP
@@ -28,14 +38,23 @@
         pl.semaphore_signal(barrier, inc=1, device_id={"rows": (me + step) % ranks}, device_id_type=MESH)
 
     span = 4 * LANES
-    tiles = words // LANES
-    flat = jnp.concatenate([hess_ref[pl.ds(j, tiles, stride=4), :] for j in range(4)], axis=1)
-    top = flat.astype(jnp.bfloat16).astype(jnp.float32)
-    rest = flat - top
     row = lax.broadcasted_iota(jnp.int32, (span, span), 0)
     col = lax.broadcasted_iota(jnp.int32, (span, span), 1)
     order = jnp.where(row == 4 * (col % LANES) + col // LANES, 1.0, 0.0).astype(jnp.bfloat16)
-    pieces = jnp.concatenate([top, rest], axis=0).astype(jnp.bfloat16)
+    hess_load.wait()
+    flat = jnp.concatenate([hess_ref[pl.ds(j, tiles, stride=4), :] for j in range(4)], axis=1)
+    right_factor = flat.astype(jnp.bfloat16).astype(jnp.float32)
+    left_factor = jnp.ones_like(flat)
+    miss = jnp.abs(flat - right_factor)
+    for j in range(1, 128, 2):
+        factor = 1.0 + j / 128.0
+        other = (flat * (1.0 / factor)).astype(jnp.bfloat16).astype(jnp.float32)
+        away = jnp.abs(flat - other * factor)
+        better = away < miss
+        left_factor = jnp.where(better, factor, left_factor)
+        right_factor = jnp.where(better, other, right_factor)
+        miss = jnp.minimum(miss, away)
+    pieces = jnp.concatenate([left_factor, right_factor], axis=0).astype(jnp.bfloat16)
     moved = jnp.dot(pieces, order, preferred_element_type=jnp.float32)
     for piece in range(2):
         for k in range(4):
@@ -44,12 +63,12 @@
                 wts[piece, k, :, t * LANES : (t + 1) * LANES] = jnp.broadcast_to(line, (GROUP, LANES)).astype(jnp.bfloat16)
 
     for t in range(tiles):
+        bins_loads[t].wait()
         cols[:, t * LANES : (t + 1) * LANES] = bins_ref[t * LANES : (t + 1) * LANES, :].T
 
     def group_hist(group):
         base = pl.multiple_of(group * GROUP, GROUP)
         zero = jnp.zeros((GROUP, CHUNK), jnp.bfloat16)
-        one = jnp.ones((GROUP, CHUNK), jnp.bfloat16)
         sums = [None, None]
         index = 0
         for c in range(words // CHUNK):
@@ -59,15 +78,13 @@
                 low = jnp.bitwise_and(jnp.right_shift(part, 8 * k), 15).astype(jnp.float32).astype(jnp.bfloat16)
                 w0 = wts[0, k, :, c * CHUNK : (c + 1) * CHUNK]
                 w1 = wts[1, k, :, c * CHUNK : (c + 1) * CHUNK]
-                hot = [high == jnp.bfloat16(h) for h in range(LEVELS)]
-                left = jnp.concatenate([jnp.where(m, w0, zero) for m in hot] + [jnp.where(m, w1, zero) for m in hot], axis=0)
-                right = jnp.concatenate([jnp.where(low == jnp.bfloat16(l), one, zero) for l in range(LEVELS)], axis=0)
+                left = jnp.concatenate([jnp.where(high == jnp.bfloat16(h), w0, zero) for h in range(LEVELS)], axis=0)
+                right = jnp.concatenate([jnp.where(low == jnp.bfloat16(l), w1, zero) for l in range(LEVELS)], axis=0)
                 part_sum = lax.dot_general(left, right, (((1,), (1,)), ((), ())), preferred_element_type=jnp.float32)
                 side = index % 2
                 sums[side] = part_sum if sums[side] is None else sums[side] + part_sum
                 index += 1
-        both = sums[0] + sums[1]
-        joint = both[:lanes] + both[lanes:]
+        joint = sums[0] + sums[1]
         own_row = lax.broadcasted_iota(jnp.int32, (GROUP, lanes), 0)
         own_col = lax.broadcasted_iota(jnp.int32, (GROUP, lanes), 1)
         keep = own_row == own_col % GROUP
@@ -128,6 +145,7 @@
     inner = inner3[:LEVELS] + inner3[LEVELS : 2 * LEVELS] + inner3[2 * LEVELS :]
     level = level3[:LEVELS] + level3[LEVELS : 2 * LEVELS] + level3[2 * LEVELS :]
     inv = 1.0 / (total + 1.0)
+    thr_load.wait()
     column = jnp.broadcast_to(thr_ref[...], (LANES, thr_ref.shape[1])).T
     whole = jnp.sum(level, axis=0, keepdims=True)
     target = column * whole[:, :LANES]
@@ -174,15 +192,19 @@
         lanes = LEVELS * GROUP
         return pl.pallas_call(
             functools.partial(kernel, ranks),
-            out_shape=jax.ShapeDtypeStruct((width, quantiles), jnp.float32),
-            in_specs=[pl.BlockSpec(memory_space=pltpu.VMEM)] * 3,
+            out_shape=pltpu.VMEM((width, quantiles), jnp.float32),
+            in_specs=[pl.BlockSpec(memory_space=pl.ANY)] * 3,
             out_specs=pl.BlockSpec(memory_space=pltpu.VMEM),
             scratch_shapes=[
+                pltpu.VMEM((words, width), jnp.int32),
+                pltpu.VMEM((4 * words // LANES, LANES), jnp.float32),
+                pltpu.VMEM((1, quantiles), jnp.float32),
                 pltpu.VMEM((width, words), jnp.int32),
                 pltpu.VMEM((2, 4, GROUP, words), jnp.bfloat16),
                 pltpu.VMEM((groups, LEVELS, lanes), jnp.float32),
                 pltpu.VMEM((ranks, LEVELS, lanes), jnp.float32),
                 pltpu.VMEM((GROUP, quantiles), jnp.float32),
+                pltpu.SemaphoreType.DMA((words // LANES + 2,)),
                 pltpu.SemaphoreType.DMA((ranks,)),
                 pltpu.SemaphoreType.DMA((ranks,)),
                 pltpu.SemaphoreType.DMA((groups,)),

time: 21.4 us -> 16.7 us (0.78)
  Pallas kernels: 19.7 us -> 15.9 us
  local copies, waits for them, and re-layouts: 1.47 us -> 0.63 us
    pallas_call x1, Pallas kernels: 19.7 us -> 15.9 us  [local(): pl.pallas_call(functools.partial(kernel, ranks), out_shape=pltpu.VMEM((wi...]
    unnamed x1, local copies, waits for them, and re-layouts: 1.47 us -> 0.63 us
where the time goes in v2:
time: 16.7 us; the launch traced here: 16.5 us
  Pallas kernels  15.9 us (95%)
  local copies, waits for them, and re-layouts  0.63 us (4%)
    pallas_call x1, Pallas kernels, local(): pl.pallas_call(functools.partial(kernel, ranks), out_shape=pltpu.VMEM((wi...  15.9 us
    unnamed x1, local copies, waits for them, and re-layouts  0.63 us

profile of v2, /device:TPU:0, one launch (start us, length us, event | category | flops | bytes accessed | tf_op | source)
XLA Modules:
  0.0 16.5 jit_solution(16358019887590565205)
XLA Ops:
  0.0 15.9 %shard_map.37 = f32[128,128]{1,0:T(8,128)S(1)} custom-call(s32[1024,128]{1,0:T(8,128)} %bins_hbm.1, f32[32,128]{1,0:T(8,128)} %bitcast.2, f32[1,128]{1,0:T(1,128)} %bitcast.3), custom_call_target="tpu_custom_call" | custom-call | tf_op jit(solution)/shard_map/pallas_call | solution.py:193
  15.9 0.6 %copy.5 = f32[128,128]{1,0:T(8,128)} copy(f32[128,128]{1,0:T(8,128)S(1)} %shard_map.37) | data formatting | bytes 131072

commit v3 on v2

--- a/solution.py
+++ b/solution.py
@@ -15,7 +15,7 @@
 MESH = pl.DeviceIdType.MESH
 
 
-def kernel(ranks, bins_hbm, hess_hbm, thr_hbm, out_ref, bins_ref, hess_ref, thr_ref, cols, wts, stage, inbox, mine, load_sem, send_sem, recv_sem, gather_send, gather_recv):
+def kernel(ranks, bins_hbm, hess_hbm, thr_hbm, out_ref, bins_ref, hess_ref, thr_ref, prefix, column_ref, cols, wts, stage, inbox, mine, load_sem, send_sem, recv_sem, gather_send, gather_recv):
     words, width = bins_ref.shape
     tiles = words // LANES
     hess_load = pltpu.make_async_copy(hess_hbm, hess_ref, load_sem.at[tiles])
@@ -37,34 +37,55 @@
     for step in range(1, ranks):
         pl.semaphore_signal(barrier, inc=1, device_id={"rows": (me + step) % ranks}, device_id_type=MESH)
 
-    span = 4 * LANES
-    row = lax.broadcasted_iota(jnp.int32, (span, span), 0)
-    col = lax.broadcasted_iota(jnp.int32, (span, span), 1)
-    order = jnp.where(row == 4 * (col % LANES) + col // LANES, 1.0, 0.0).astype(jnp.bfloat16)
+    src = lax.broadcasted_iota(jnp.int32, (lanes, lanes), 0)
+    dst = lax.broadcasted_iota(jnp.int32, (lanes, lanes), 1)
+    gap = dst - src
+    same = jnp.bitwise_and(gap, GROUP - 1) == 0
+    prefix[:, :lanes] = jnp.where(jnp.logical_and(same, gap > 0), 1.0, 0.0).astype(jnp.bfloat16)
+    prefix[:, lanes:] = jnp.where(same, 1.0, 0.0).astype(jnp.bfloat16)
+
+    row = lax.broadcasted_iota(jnp.int32, (LANES, LANES), 0)
+    col = lax.broadcasted_iota(jnp.int32, (LANES, LANES), 1)
+    quarter = LANES // 4
+    order = jnp.where(row == 4 * (col % quarter) + col // quarter, 1.0, 0.0).astype(jnp.bfloat16)
+    lane = lax.broadcasted_iota(jnp.int32, (2 * tiles, LANES), 1) // quarter
     hess_load.wait()
-    flat = jnp.concatenate([hess_ref[pl.ds(j, tiles, stride=4), :] for j in range(4)], axis=1)
-    right_factor = flat.astype(jnp.bfloat16).astype(jnp.float32)
+    for t in range(tiles):
+        bins_loads[t].wait()
+    thr_load.wait()
+    for t in range(tiles):
+        cols[:, t * LANES : (t + 1) * LANES] = bins_ref[t * LANES : (t + 1) * LANES, :].T
+    column_ref[...] = jnp.broadcast_to(thr_ref[...], (LANES, thr_ref.shape[1])).T
+    flat = jnp.concatenate([hess_ref[pl.ds(j, tiles, stride=4), :] for j in range(4)], axis=0)
     left_factor = jnp.ones_like(flat)
-    miss = jnp.abs(flat - right_factor)
+    miss = jnp.abs(flat - flat.astype(jnp.bfloat16).astype(jnp.float32))
     for j in range(1, 128, 2):
         factor = 1.0 + j / 128.0
         other = (flat * (1.0 / factor)).astype(jnp.bfloat16).astype(jnp.float32)
         away = jnp.abs(flat - other * factor)
-        better = away < miss
-        left_factor = jnp.where(better, factor, left_factor)
-        right_factor = jnp.where(better, other, right_factor)
+        left_factor = jnp.where(away < miss, factor, left_factor)
         miss = jnp.minimum(miss, away)
-    pieces = jnp.concatenate([left_factor, right_factor], axis=0).astype(jnp.bfloat16)
-    moved = jnp.dot(pieces, order, preferred_element_type=jnp.float32)
-    for piece in range(2):
-        for k in range(4):
+    right_factor = flat / left_factor
+    pieces = jnp.concatenate([x[j * tiles : (j + 1) * tiles] for j in range(4) for x in (left_factor, right_factor)], axis=0)
+    moved = jnp.dot(pieces.astype(jnp.bfloat16), order, preferred_element_type=jnp.float32)
+    for k in range(4):
+        plane = None
+        for j in range(4):
+            block = moved[2 * tiles * j : 2 * tiles * (j + 1)]
+            if j != k:
+                block = pltpu.roll(block, (quarter * (j - k)) % LANES, 1)
+            plane = block if plane is None else jnp.where(lane == j, block, plane)
+        for piece in range(2):
             for t in range(tiles):
-                line = moved[piece * tiles + t : piece * tiles + t + 1, k * LANES : (k + 1) * LANES]
+                line = plane[piece * tiles + t : piece * tiles + t + 1]
                 wts[piece, k, :, t * LANES : (t + 1) * LANES] = jnp.broadcast_to(line, (GROUP, LANES)).astype(jnp.bfloat16)
 
-    for t in range(tiles):
-        bins_loads[t].wait()
-        cols[:, t * LANES : (t + 1) * LANES] = bins_ref[t * LANES : (t + 1) * LANES, :].T
+    def peer(step):
+        place, bit = 0, 1
+        while bit < groups:
+            place = place + (seat // bit + step // bit) % 2 * bit
+            bit *= 2
+        return place
 
     def group_hist(group):
         base = pl.multiple_of(group * GROUP, GROUP)
@@ -94,7 +115,7 @@
         return jnp.concatenate(lines, axis=0)
 
     def outgoing(step, e):
-        target = ((team + e) % replicas) * groups + (seat + step) % groups
+        target = ((team + e) % replicas) * groups + peer(step)
         slot = step * replicas + e
         return pltpu.make_async_remote_copy(
             src_ref=stage.at[step],
@@ -106,8 +127,8 @@
         )
 
     def do_group(turn, carry):
-        step = (turn + 1) % groups
-        stage[step] = group_hist((seat + step) % groups)
+        step = groups - 1 - turn
+        stage[step] = group_hist(peer(step))
 
         @pl.when(turn == 0)
         def _():
@@ -125,30 +146,23 @@
         outgoing(0, e).start()
 
     total = stage[0]
-    for step in range(groups):
+    for step in reversed(range(groups)):
         for e in range(replicas):
             if step + e > 0:
                 outgoing(step, e).wait()
                 total = total + inbox[step * replicas + e]
 
-    src = lax.broadcasted_iota(jnp.int32, (lanes, lanes), 0)
-    dst = lax.broadcasted_iota(jnp.int32, (lanes, lanes), 1)
-    same = src % GROUP == dst % GROUP
-    earlier = jnp.where(jnp.logical_and(same, src < dst), 1.0, 0.0).astype(jnp.bfloat16)
-    every = jnp.where(same, 1.0, 0.0).astype(jnp.bfloat16)
     p0 = total.astype(jnp.bfloat16).astype(jnp.float32)
     p1 = (total - p0).astype(jnp.bfloat16).astype(jnp.float32)
     p2 = total - p0 - p1
     split = jnp.concatenate([p0, p1, p2], axis=0).astype(jnp.bfloat16)
-    inner3 = jnp.dot(split, earlier, preferred_element_type=jnp.float32)
-    level3 = jnp.dot(split, every, preferred_element_type=jnp.float32)
+    sums3 = jnp.dot(split, prefix[...], preferred_element_type=jnp.float32)
+    inner3, level3 = sums3[:, :lanes], sums3[:, lanes:]
     inner = inner3[:LEVELS] + inner3[LEVELS : 2 * LEVELS] + inner3[2 * LEVELS :]
     level = level3[:LEVELS] + level3[LEVELS : 2 * LEVELS] + level3[2 * LEVELS :]
     inv = 1.0 / (total + 1.0)
-    thr_load.wait()
-    column = jnp.broadcast_to(thr_ref[...], (LANES, thr_ref.shape[1])).T
     whole = jnp.sum(level, axis=0, keepdims=True)
-    target = column * whole[:, :LANES]
+    target = column_ref[...] * whole[:, :LANES]
     run = jnp.zeros((1, lanes), jnp.float32)
     acc = jnp.zeros((thr_ref.shape[1], LANES), jnp.float32)
     for h in range(LEVELS):
@@ -171,11 +185,11 @@
             dst_ref=out_ref.at[pl.ds(here, GROUP), :],
             send_sem=gather_send.at[step],
             recv_sem=gather_recv.at[step],
-            device_id={"rows": team * groups + (seat + step) % groups},
+            device_id={"rows": team * groups + peer(step)},
             device_id_type=MESH,
         )
 
-    for step in range(1, groups):
+    for step in reversed(range(1, groups)):
         spread(step).start()
     out_ref[pl.ds(here, GROUP), :] = cuts
     for step in range(1, groups):
@@ -199,6 +213,8 @@
                 pltpu.VMEM((words, width), jnp.int32),
                 pltpu.VMEM((4 * words // LANES, LANES), jnp.float32),
                 pltpu.VMEM((1, quantiles), jnp.float32),
+                pltpu.VMEM((lanes, 2 * lanes), jnp.bfloat16),
+                pltpu.VMEM((quantiles, LANES), jnp.float32),
                 pltpu.VMEM((width, words), jnp.int32),
                 pltpu.VMEM((2, 4, GROUP, words), jnp.bfloat16),
                 pltpu.VMEM((groups, LEVELS, lanes), jnp.float32),

time: 16.7 us -> 16.2 us (0.970)
  Pallas kernels: 15.9 us -> 15.4 us
    pallas_call x1, Pallas kernels: 15.9 us -> 15.4 us  [local(): pl.pallas_call(functools.partial(kernel, ranks), out_shape=pltpu.VMEM((wi...]
where the time goes in v3:
time: 16.2 us; the launch traced here: 16 us
  Pallas kernels  15.4 us (95%)
  local copies, waits for them, and re-layouts  0.63 us (4%)
    pallas_call x1, Pallas kernels, local(): pl.pallas_call(functools.partial(kernel, ranks), out_shape=pltpu.VMEM((wi...  15.4 us
    unnamed x1, local copies, waits for them, and re-layouts  0.63 us

profile of v3, /device:TPU:0, one launch (start us, length us, event | category | flops | bytes accessed | tf_op | source)
XLA Modules:
  0.0 16.0 jit_solution(12048527020280133626)
XLA Ops:
  0.0 15.4 %shard_map.37 = f32[128,128]{1,0:T(8,128)S(1)} custom-call(s32[1024,128]{1,0:T(8,128)} %bins_hbm.1, f32[32,128]{1,0:T(8,128)} %bitcast.2, f32[1,128]{1,0:T(1,128)} %bitcast.3), custom_call_target="tpu_custom_call" | custom-call | tf_op jit(solution)/shard_map/pallas_call | solution.py:207
  15.4 0.6 %copy.5 = f32[128,128]{1,0:T(8,128)} copy(f32[128,128]{1,0:T(8,128)S(1)} %shard_map.37) | data formatting | bytes 131072

commit v4 on v3

--- a/solution.py
+++ b/solution.py
@@ -50,12 +50,6 @@
     order = jnp.where(row == 4 * (col % quarter) + col // quarter, 1.0, 0.0).astype(jnp.bfloat16)
     lane = lax.broadcasted_iota(jnp.int32, (2 * tiles, LANES), 1) // quarter
     hess_load.wait()
-    for t in range(tiles):
-        bins_loads[t].wait()
-    thr_load.wait()
-    for t in range(tiles):
-        cols[:, t * LANES : (t + 1) * LANES] = bins_ref[t * LANES : (t + 1) * LANES, :].T
-    column_ref[...] = jnp.broadcast_to(thr_ref[...], (LANES, thr_ref.shape[1])).T
     flat = jnp.concatenate([hess_ref[pl.ds(j, tiles, stride=4), :] for j in range(4)], axis=0)
     left_factor = jnp.ones_like(flat)
     miss = jnp.abs(flat - flat.astype(jnp.bfloat16).astype(jnp.float32))
@@ -66,6 +60,12 @@
         left_factor = jnp.where(away < miss, factor, left_factor)
         miss = jnp.minimum(miss, away)
     right_factor = flat / left_factor
+    for t in range(tiles):
+        bins_loads[t].wait()
+    thr_load.wait()
+    for t in range(tiles):
+        cols[:, t * LANES : (t + 1) * LANES] = bins_ref[t * LANES : (t + 1) * LANES, :].T
+    column_ref[...] = jnp.broadcast_to(thr_ref[...], (LANES, thr_ref.shape[1])).T
     pieces = jnp.concatenate([x[j * tiles : (j + 1) * tiles] for j in range(4) for x in (left_factor, right_factor)], axis=0)
     moved = jnp.dot(pieces.astype(jnp.bfloat16), order, preferred_element_type=jnp.float32)
     for k in range(4):
@@ -126,22 +126,28 @@
             device_id_type=MESH,
         )
 
-    def do_group(turn, carry):
-        step = groups - 1 - turn
-        stage[step] = group_hist(peer(step))
+    def do_pair(turn, carry):
+        step = groups - 1 - 2 * turn
+        first = group_hist(peer(step))
+        second = group_hist(peer(step - 1))
+        stage[step] = first
+        stage[step - 1] = second
 
         @pl.when(turn == 0)
         def _():
             pl.semaphore_wait(barrier, ranks - 1)
 
-        @pl.when(turn < groups - 1)
+        for e in range(replicas):
+            outgoing(step, e).start()
+
+        @pl.when(turn < groups // 2 - 1)
         def _():
             for e in range(replicas):
-                outgoing(step, e).start()
+                outgoing(step - 1, e).start()
 
         return carry
 
-    lax.fori_loop(0, groups, do_group, 0)
+    lax.fori_loop(0, groups // 2, do_pair, 0)
     for e in range(1, replicas):
         outgoing(0, e).start()
 

time: 16.2 us -> 15.4 us (0.951)
  Pallas kernels: 15.4 us -> 14.5 us
    pallas_call x1, Pallas kernels: 15.4 us -> 14.5 us  [local(): pl.pallas_call(functools.partial(kernel, ranks), out_shape=pltpu.VMEM((wi...]
where the time goes in v4:
time: 15.4 us; the launch traced here: 15.2 us
  Pallas kernels  14.5 us (94%)
  local copies, waits for them, and re-layouts  0.63 us (4%)
    pallas_call x1, Pallas kernels, local(): pl.pallas_call(functools.partial(kernel, ranks), out_shape=pltpu.VMEM((wi...  14.5 us
    unnamed x1, local copies, waits for them, and re-layouts  0.63 us

profile of v4, /device:TPU:0, one launch (start us, length us, event | category | flops | bytes accessed | tf_op | source)
XLA Modules:
  0.0 15.2 jit_solution(13601032401176783040)
XLA Ops:
  0.0 14.5 %shard_map.37 = f32[128,128]{1,0:T(8,128)S(1)} custom-call(s32[1024,128]{1,0:T(8,128)} %bins_hbm.1, f32[32,128]{1,0:T(8,128)} %bitcast.2, f32[1,128]{1,0:T(1,128)} %bitcast.3), custom_call_target="tpu_custom_call" | custom-call | tf_op jit(solution)/shard_map/pallas_call | solution.py:213
  14.5 0.6 %copy.5 = f32[128,128]{1,0:T(8,128)} copy(f32[128,128]{1,0:T(8,128)S(1)} %shard_map.37) | data formatting | bytes 131072
